TPU v7x, 32 devices: a whole 2x2x4 slice. The times are simulated.
32 devices in a mesh: rep: 2 (over x), shard: 16 (over z, y, core).
Axes of the slice: x: 2, y: 2, z: 4, core: 2. Of those that a mesh axis runs over, the one named last changes fastest.
Arguments:
- hidden: bfloat16 [12288, 64], P(('rep', 'shard')), may hold values from -6 to 6
- grad_out: bfloat16 [12288, 4096], P(('rep', 'shard')), may hold values from -6 to 6
- weight_band: bfloat16 [64, 4096], P('shard'), may hold values from -0.09375 to 0.09375
- error_feedback: float32 [2, 64, 4096], P('rep', 'shard'), may hold values from -4.2426405 to 4.2426405
- q_start: float32 [4096, 32], replicated, may hold values from -6 to 6
Outputs:
- update: float32 [64, 4096], P('shard')
- error_next: float32 [2, 64, 4096], P('rep', 'shard')
- q_next: float32 [4096, 32], replicated
- d_hidden: bfloat16 [12288, 64], P(('rep', 'shard'))
All inputs are finite; a program needn't handle non-finite values.
Results may differ from a plain program's by a relative error of at most 0.0004.
Values may be sent and summed in bfloat16 or wider, within the bound.
A program may use at most 64 MiB of HBM per device.

v0:
```python
import math
import jax
import jax.numpy as jnp
from jax import lax
from jax.sharding import PartitionSpec as P

POWER = 2


def orthonormal(matrix):
    gram_matrix = jnp.dot(matrix.T, matrix, precision=lax.Precision.HIGHEST)
    factor_low = jnp.linalg.cholesky(gram_matrix)
    return lax.linalg.triangular_solve(
        factor_low, matrix, left_side=False, lower=True, transpose_a=True
    )


def orth_rows(p_local):
    all_rows = lax.all_gather(p_local, "shard", axis=0, tiled=True)
    gram_matrix = jnp.dot(all_rows.T, all_rows, precision=lax.Precision.HIGHEST)
    factor_low = jnp.linalg.cholesky(gram_matrix)
    return lax.linalg.triangular_solve(
        factor_low, p_local, left_side=False, lower=True, transpose_a=True
    )


def body(hidden, grad_out, weight_band, error_feedback, q_start):
    n_rep = lax.axis_size("rep")
    n_shard = lax.axis_size("shard")
    token_rows = hidden.shape[0]
    grad_scale = 1.0 / math.sqrt(token_rows * n_shard * n_rep)
    d_hidden = lax.dot_general(
        grad_out,
        lax.all_gather(weight_band, "shard", axis=0, tiled=True),
        (((1,), (1,)), ((), ())),
        preferred_element_type=jnp.float32,
    ).astype(jnp.bfloat16)
    grad_rows = lax.psum_scatter(
        lax.dot_general(
            hidden, grad_out, (((0,), (0,)), ((), ())), preferred_element_type=jnp.float32
        )
        * grad_scale,
        "shard",
        scatter_dimension=0,
        tiled=True,
    )
    own_rows = grad_rows + error_feedback[0]
    q_factor = q_start
    p_factor = None
    for round_index in range(POWER):
        q_hat = orthonormal(q_factor)
        p_local = jnp.dot(own_rows, q_hat, precision=lax.Precision.HIGHEST)
        p_factor = orth_rows(lax.psum(p_local, "rep"))
        q_term = lax.dot_general(
            own_rows, p_factor, (((0,), (0,)), ((), ())), precision=lax.Precision.HIGHEST
        )
        q_factor = lax.psum(q_term, ("rep", "shard"))
    update = jnp.dot(p_factor, q_factor.T, precision=lax.Precision.HIGHEST)
    error_next = own_rows - update / n_rep
    return (update, error_next[None], q_factor, d_hidden)


def solution(mesh):
    return jax.shard_map(
        body,
        mesh=mesh,
        in_specs=(
            P(("rep", "shard"), None),
            P(("rep", "shard"), None),
            P("shard", None),
            P("rep", "shard", None),
            P(),
        ),
        out_specs=(P("shard", None), P("rep", "shard", None), P(), P(("rep", "shard"), None)),
        check_vma=False,
    )
```

profile of v0, /device:TPU:0, one launch (start us, length us, event | category | flops | bytes accessed | tf_op | source)
XLA Modules:
  0.0 451.4 jit_solution(12840853244050156011)
XLA Ops:
  7.2 1.8 copy-done
  9.1 2.5 convolution_multiply_fusion
  11.6 1.8 fusion.18
  13.4 0.1 copy.13
  13.5 2.9 cholesky.74
  16.5 0.6 compare_reduce_fusion.3
  17.1 0.7 fusion
  17.8 2.4 custom-call.10
  20.2 0.6 dynamic-slice
  21.5 2.5 convolution_bitcast_fusion.1
  23.9 84.3 %all-reduce.9.cloned.1.call-done = f32[64,4096]{1,0:T(8,128)} async-done(((f32[64,4096]{1,0:T(8,128)}), f32[64,4096]{1,0:T(8,128)}) %all-reduce.9.cloned.1.call-update) | async-done | bytes 1048592
  108.3 0.9 dynamic-slice_add_fusion
  109.2 1.6 fusion.19
  110.7 4.9 %psum.28 = f32[4,32]{1,0:T(4,128)S(1)} all-reduce(f32[4,32]{1,0:T(4,128)S(1)} %fusion.19), channel_id=1, replica_groups=mesh['rep'=2,'shard'=16] {'rep'}, use_global_device_ids=true, to_apply=%region_3.6 | all-reduce | flops 128 | bytes 1024 | tf_op jit(solution)/shard_map/psum | solution.py:53
  115.7 19.5 %all-gather = f32[16,4,32]{2,1,0:T(4,128)S(1)} all-gather(f32[1,4,32]{2,1,0:T(4,128)S(1)} %bitcast.83), channel_id=1, replica_groups=mesh['rep'=2,'shard'=16] {'shard'}, dimensions={0}, use_global_device_ids=true | all-gather | bytes 8704 | tf_op jit(solution)/shard_map/all_gather | solution.py:19
  135.2 0.2 fusion.20
  135.4 0.1 copy.14
  135.5 2.9 cholesky.85
  138.4 0.6 compare_reduce_fusion.2
  139.1 0.7 fusion.1
  139.7 2.5 custom-call.11
  142.2 0.2 convolution_bitcast_fusion.2
  142.4 1.3 fusion.21
  143.9 20.5 %all-gather.2 = bf16[16,4,4096]{2,1,0:T(4,128)(2,1)} all-gather(bf16[1,4,4096]{2,1,0:T(4,128)(2,1)S(1)} %bitcast.82), channel_id=1, replica_groups=mesh['rep'=2,'shard'=16] {'shard'}, dimensions={0}, use_global_device_ids=true | all-gather | bytes 557056 | tf_op jit(solution)/shard_map/all_gather | solution.py:34
  164.4 2.0 reshape.34
  166.3 104.4 %all-reduce.5.cloned.1.call-done = f32[4096,32]{0,1:T(8,128)} async-done(((f32[4096,32]{0,1:T(8,128)}), f32[4096,32]{0,1:T(8,128)}) %all-reduce.5.cloned.1.call-update) | async-done | bytes 524304 | tf_op jit(solution)/shard_map/psum | solution.py:57
  270.7 1.8 fusion.22
  272.5 2.9 cholesky.96
  275.5 0.6 compare_reduce_fusion.1
  276.1 0.7 fusion.2
  276.8 2.4 custom-call.12
  279.2 1.7 convolution_bitcast_fusion
  280.9 0.5 fusion.23
  281.4 4.9 %psum.30 = f32[4,32]{1,0:T(4,128)S(1)} all-reduce(f32[4,32]{1,0:T(4,128)S(1)} %fusion.23), channel_id=1, replica_groups=mesh['rep'=2,'shard'=16] {'rep'}, use_global_device_ids=true, to_apply=%region_5.9 | all-reduce | flops 128 | bytes 1024 | tf_op jit(solution)/shard_map/psum | solution.py:53
  286.4 20.4 %all-gather.1 = f32[16,4,32]{2,1,0:T(4,128)S(1)} all-gather(f32[1,4,32]{2,1,0:T(4,128)S(1)} %bitcast.84), channel_id=1, replica_groups=mesh['rep'=2,'shard'=16] {'shard'}, dimensions={0}, use_global_device_ids=true | all-gather | bytes 8704 | tf_op jit(solution)/shard_map/all_gather | solution.py:19
  306.7 0.2 fusion.24
  307.0 0.1 copy.16
  307.0 2.9 cholesky.107
  310.0 0.6 compare_reduce_fusion
  310.6 0.7 fusion.3
  311.3 2.5 custom-call.13
  313.8 0.1 convolution_bitcast_fusion.3
  313.9 1.4 fusion.25
  315.3 2.7 convolution_convert_fusion
  318.1 122.9 %all-reduce.7.cloned.1.call-done = f32[4096,32]{0,1:T(8,128)} async-done(((f32[4096,32]{0,1:T(8,128)}), f32[4096,32]{0,1:T(8,128)}) %all-reduce.7.cloned.1.call-update) | async-done | bytes 524304 | tf_op jit(solution)/shard_map/psum | solution.py:57
  441.0 1.4 fusion.26
  442.4 0.7 subtract_bitcast_fusion
  443.0 1.9 copy.20
  (24 shorter events, 0.4 us)
Async XLA Ops:
  7.2 1.9 copy-start
  7.2 13.0 %copy-start.4 = (u32[32]{0:T(128)S(1)}, u32[32]{0:T(128)}, u32[]{:S(2)}) copy-start(u32[32]{0:T(128)} %constant.41) | copy-start | bytes 388
  7.2 101.1 %copy-start.2 = (f32[1,4,4096]{2,1,0:T(4,128)S(1)}, f32[1,4,4096]{2,1,0:T(4,128)}, u32[]{:S(2)}) copy-start(f32[1,4,4096]{2,1,0:T(4,128)} %param.13) | copy-start | bytes 196612
  7.2 101.1 %all-reduce.9.cloned.1.call-start = ((), (), s32[]{:S(2)}) async-start(), calls=%async_computation.2 | async-start | bytes 2097152
  11.6 132.3 %copy-start.3 = (bf16[4,4096]{1,0:T(4,128)(2,1)S(1)}, bf16[4,4096]{1,0:T(4,128)(2,1)}, u32[]{:S(2)}) copy-start(bf16[4,4096]{1,0:T(4,128)(2,1)} %param.12) | copy-start | bytes 98308
  11.6 259.1 %all-reduce.5.cloned.1.call-start = ((), (), s32[]{:S(2)}) async-start(), calls=%async_computation | async-start | bytes 1048576 | tf_op jit(solution)/shard_map/psum | solution.py:57
  143.8 297.2 %all-reduce.7.cloned.1.call-start = ((), (), s32[]{:S(2)}) async-start(), calls=%async_computation.1 | async-start | bytes 1048576 | tf_op jit(solution)/shard_map/psum | solution.py:57
  442.4 2.5 copy-start.1
Sparse Core Ops, SparseCore 0:
  11.7 96.4 all-reduce.8
  143.9 126.7 all-reduce.4
  315.5 125.4 all-reduce.6
where the time goes:
time: 452 us; the launch traced here: 451 us
  waiting for transfers between devices  312 us (69%)
  blocking collectives  70.2 us (16%)
  other arithmetic  28.4 us (6%)
  matrix products  19.9 us (4%)
  between operations  14.6 us (3%)
  local copies, waits for them, and re-layouts  6.59 us (1%)
    psum x2, waiting for transfers between devices, body(): q_factor = lax.psum(q_term, ('rep', 'shard'))  227 us
    unnamed x4, waiting for transfers between devices  84.4 us
    all_gather x2, blocking collectives, orth_rows(): all_rows = lax.all_gather(p_local, 'shard', axis=0, tiled=True)  39.9 us
    all_gather x1, blocking collectives, body(): lax.all_gather(weight_band, 'shard', axis=0, tiled=True)  20.5 us
    psum x2, blocking collectives, body(): p_factor = orth_rows(lax.psum(p_local, 'rep'))  9.85 us
  transfers between devices with their start and end apart: 3, of which 3 were waited for; matrix products, arithmetic and copies ran while one was open for 4% of the time, Pallas kernels for 0%

commit v1 on v0

--- a/solution.py
+++ b/solution.py
@@ -54,7 +54,7 @@
         q_term = lax.dot_general(
             own_rows, p_factor, (((0,), (0,)), ((), ())), precision=lax.Precision.HIGHEST
         )
-        q_factor = lax.psum(q_term, ("rep", "shard"))
+        q_factor = jnp.sum(lax.all_gather(q_term, ("rep", "shard")), axis=0)
     update = jnp.dot(p_factor, q_factor.T, precision=lax.Precision.HIGHEST)
     error_next = own_rows - update / n_rep
     return (update, error_next[None], q_factor, d_hidden)

time: 452 us -> 475 us (1.051)
  local copies, waits for them, and re-layouts: 6.59 us -> 40.1 us
  waiting for transfers between devices: 312 us -> 282 us
  other arithmetic: 28.4 us -> 47 us
    psum x2 -> x0, waiting for transfers between devices: 227 us -> none  [body(): q_factor = lax.psum(q_term, ('rep', 'shard'))]
    all_gather x0 -> x2, waiting for transfers between devices: none -> 197 us  [body(): q_factor = jnp.sum(lax.all_gather(q_term, ('rep', 'shard')), axis=0)]
    unnamed x13 -> x16, local copies, waits for them, and re-layouts: 6.29 us -> 39.8 us
    reduce_sum x0 -> x2, other arithmetic: none -> 18.6 us  [body(): q_factor = jnp.sum(lax.all_gather(q_term, ('rep', 'shard')), axis=0)]
  transfers between devices with their start and end apart: 3 -> 3, of which waited for: 3 -> 3; matrix products, arithmetic and copies ran while one was open for 4% -> 3% of each run, Pallas kernels for 0% -> 0%
where the time goes in v1:
time: 475 us
  waiting for transfers between devices  282 us (59%)
  blocking collectives  70.8 us (15%)
  other arithmetic  47 us (10%)
  local copies, waits for them, and re-layouts  40.1 us (8%)
  matrix products  20.1 us (4%)
  between operations  14.6 us (3%)
    all_gather x2, waiting for transfers between devices, body(): q_factor = jnp.sum(lax.all_gather(q_term, ('rep', 'shard')), axis=0)  197 us
    unnamed x4, waiting for transfers between devices  84.3 us
    unnamed x16, local copies, waits for them, and re-layouts  39.8 us
    all_gather x2, blocking collectives, orth_rows(): all_rows = lax.all_gather(p_local, 'shard', axis=0, tiled=True)  39.2 us
    all_gather x1, blocking collectives, body(): lax.all_gather(weight_band, 'shard', axis=0, tiled=True)  21.8 us
    reduce_sum x2, other arithmetic, body(): q_factor = jnp.sum(lax.all_gather(q_term, ('rep', 'shard')), axis=0)  18.6 us
    psum x2, blocking collectives, body(): p_factor = orth_rows(lax.psum(p_local, 'rep'))  9.85 us
  transfers between devices with their start and end apart: 3, of which 3 were waited for; matrix products, arithmetic and copies ran while one was open for 3% of the time, Pallas kernels for 0%

profile of v1, /device:TPU:0, one launch (start us, length us, event | category | flops | bytes accessed | tf_op | source)
XLA Modules:
  0.0 474.6 jit_solution(15815772653932079007)
XLA Ops:
  7.3 1.8 copy-done
  9.1 2.5 convolution_multiply_fusion
  11.6 1.8 fusion.18
  13.6 2.9 cholesky.74
  16.5 0.6 compare_reduce_fusion.3
  17.2 0.7 fusion
  17.8 2.4 custom-call.10
  20.2 0.6 dynamic-slice
  21.5 2.5 convolution_bitcast_fusion.1
  24.0 84.2 %all-reduce.3.cloned.1.call-done = f32[64,4096]{1,0:T(8,128)} async-done(((f32[64,4096]{1,0:T(8,128)}), f32[64,4096]{1,0:T(8,128)}) %all-reduce.3.cloned.1.call-update) | async-done | bytes 1048592
  108.2 0.9 dynamic-slice_add_fusion
  109.1 1.6 fusion.19
  110.7 4.9 %psum.14 = f32[4,32]{1,0:T(4,128)S(1)} all-reduce(f32[4,32]{1,0:T(4,128)S(1)} %fusion.19), channel_id=1, replica_groups=mesh['rep'=2,'shard'=16] {'rep'}, use_global_device_ids=true, to_apply=%region_3.6 | all-reduce | flops 128 | bytes 1024 | tf_op jit(solution)/shard_map/psum | solution.py:53
  115.6 19.5 %all-gather.2 = f32[16,4,32]{2,1,0:T(4,128)S(1)} all-gather(f32[1,4,32]{2,1,0:T(4,128)S(1)} %bitcast.95), channel_id=1, replica_groups=mesh['rep'=2,'shard'=16] {'shard'}, dimensions={0}, use_global_device_ids=true | all-gather | bytes 8704 | tf_op jit(solution)/shard_map/all_gather | solution.py:19
  135.1 0.2 fusion.20
  135.4 2.9 cholesky.85
  138.4 0.6 compare_reduce_fusion.2
  139.0 0.7 fusion.1
  139.7 2.4 custom-call.11
  142.1 0.2 convolution_bitcast_fusion.2
  142.4 1.3 fusion.21
  143.7 0.2 all-gather.10.cloned.1.call-start
  144.0 111.4 %all-gather.8.cloned.1.call-done = f32[131072,32]{0,1:T(8,128)} async-done(((f32[4096,32]{0,1:T(8,128)}), f32[131072,32]{0,1:T(8,128)}) %all-gather.8.cloned.1.call-update) | async-done | bytes 16777232 | tf_op jit(solution)/shard_map/all_gather | solution.py:57
  255.4 17.7 %copy.17 = f32[4,8,32,4096]{3,2,1,0:T(8,128)} copy(f32[4,8,32,4096]{3,1,2,0:T(8,128)} %bitcast.91) | data formatting | bytes 33554432
  273.1 9.2 %bitcast_reduce_fusion.1 = f32[4096,32]{0,1:T(8,128)} fusion(f32[4,8,32,4096]{3,2,1,0:T(8,128)} %copy.17), kind=kLoop, calls=%fused_computation.1 | loop fusion | flops 4063232 | bytes 17301504 | tf_op jit(solution)/shard_map/reduce_sum | solution.py:57
  282.3 1.8 fusion.22
  284.2 2.9 cholesky.96
  287.2 0.6 compare_reduce_fusion.1
  287.8 0.7 fusion.2
  288.5 2.4 custom-call.12
  290.9 1.7 convolution_bitcast_fusion
  292.6 0.5 fusion.23
  293.1 4.9 %psum.15 = f32[4,32]{1,0:T(4,128)S(1)} all-reduce(f32[4,32]{1,0:T(4,128)S(1)} %fusion.23), channel_id=1, replica_groups=mesh['rep'=2,'shard'=16] {'rep'}, use_global_device_ids=true, to_apply=%region_5.9 | all-reduce | flops 128 | bytes 1024 | tf_op jit(solution)/shard_map/psum | solution.py:53
  298.1 19.7 %all-gather.3 = f32[16,4,32]{2,1,0:T(4,128)S(1)} all-gather(f32[1,4,32]{2,1,0:T(4,128)S(1)} %bitcast.96), channel_id=1, replica_groups=mesh['rep'=2,'shard'=16] {'shard'}, dimensions={0}, use_global_device_ids=true | all-gather | bytes 8704 | tf_op jit(solution)/shard_map/all_gather | solution.py:19
  317.7 0.2 fusion.24
  318.0 2.9 cholesky.107
  321.0 0.6 compare_reduce_fusion
  321.6 0.7 fusion.3
  322.3 2.4 custom-call.13
  324.9 1.4 fusion.25
  326.3 21.8 %all-gather.4 = bf16[16,4,4096]{2,1,0:T(4,128)(2,1)} all-gather(bf16[1,4,4096]{2,1,0:T(4,128)(2,1)S(1)} %bitcast.94), channel_id=1, replica_groups=mesh['rep'=2,'shard'=16] {'shard'}, dimensions={0}, use_global_device_ids=true | all-gather | bytes 557056 | tf_op jit(solution)/shard_map/all_gather | solution.py:34
  348.1 2.0 reshape.36
  350.1 2.8 convolution_convert_fusion
  352.9 86.0 %all-gather.10.cloned.1.call-done = f32[131072,32]{0,1:T(8,128)} async-done(((f32[4096,32]{0,1:T(8,128)}), f32[131072,32]{0,1:T(8,128)}) %all-gather.10.cloned.1.call-update) | async-done | bytes 16777232 | tf_op jit(solution)/shard_map/all_gather | solution.py:57
  438.9 17.7 %copy.18 = f32[4,8,32,4096]{3,2,1,0:T(8,128)} copy(f32[4,8,32,4096]{3,1,2,0:T(8,128)} %bitcast.90) | data formatting | bytes 33554432
  456.6 9.4 %bitcast_reduce_fusion = f32[4096,32]{0,1:T(8,128)} fusion(f32[4,8,32,4096]{3,2,1,0:T(8,128)} %copy.18), kind=kLoop, calls=%fused_computation | loop fusion | flops 4063232 | bytes 17301504 | tf_op jit(solution)/shard_map/reduce_sum | solution.py:57
  466.0 1.4 fusion.26
  467.4 0.7 subtract_bitcast_fusion
  (29 shorter events, 0.8 us)
Async XLA Ops:
  7.2 1.9 copy-start
  7.2 13.1 %copy-start.5 = (u32[32]{0:T(128)S(1)}, u32[32]{0:T(128)}, u32[]{:S(2)}) copy-start(u32[32]{0:T(128)} %constant.43) | copy-start | bytes 388
  7.2 101.0 %copy-start.3 = (f32[1,4,4096]{2,1,0:T(4,128)S(1)}, f32[1,4,4096]{2,1,0:T(4,128)}, u32[]{:S(2)}) copy-start(f32[1,4,4096]{2,1,0:T(4,128)} %param.13) | copy-start | bytes 196612
  7.2 101.0 %all-reduce.3.cloned.1.call-start = ((), (), s32[]{:S(2)}) async-start(), calls=%async_computation.2 | async-start | bytes 2097152
  11.6 243.8 %all-gather.8.cloned.1.call-start = ((), (), s32[]{:S(2)}) async-start(), calls=%async_computation | async-start | bytes 17301504 | tf_op jit(solution)/shard_map/all_gather | solution.py:57
  143.7 295.1 %all-gather.10.cloned.1.call-start = ((), (), s32[]{:S(2)}) async-start(), calls=%async_computation.1 | async-start | bytes 17301504 | tf_op jit(solution)/shard_map/all_gather | solution.py:57
  282.3 44.0 %copy-start.4 = (bf16[4,4096]{1,0:T(4,128)(2,1)S(1)}, bf16[4,4096]{1,0:T(4,128)(2,1)}, u32[]{:S(2)}) copy-start(bf16[4,4096]{1,0:T(4,128)(2,1)} %param.12) | copy-start | bytes 98308
  456.6 11.5 %copy-start.1 = (bf16[384,4096]{1,0:T(8,128)(2,1)S(1)}, bf16[384,4096]{1,0:T(8,128)(2,1)}, u32[]{:S(2)}) copy-start(bf16[384,4096]{1,0:T(8,128)(2,1)} %param.11) | copy-start | bytes 9437188
  467.4 0.7 copy-start.2
Sparse Core Ops, SparseCore 0:
  11.7 96.4 all-reduce.2
  143.9 111.5 all-gather.7
  326.4 112.4 all-gather.9
